TPU v7x, 32 devices: a whole 2x2x4 slice. The times are simulated.
32 devices in a mesh: groups: 1, seq: 1, row: 16 (over z, y, core), col: 2 (over x).
Axes of the slice: x: 2, y: 2, z: 4, core: 2. Of those that a mesh axis runs over, the one named last changes fastest.
Arguments:
- paired_left: bfloat16 [512, 32, 512], P(('groups', 'seq', 'col'), None, 'row'), may hold values from -24 to 24
- paired_right: bfloat16 [512, 32, 512], P(('groups', 'seq', 'row'), None, 'col'), may hold values from -24 to 24
- unpaired_left: bfloat16 [1024, 32, 512], P(('groups', 'seq', 'col'), None, 'row'), may hold values from -24 to 24
- unpaired_right: bfloat16 [1024, 32, 512], P(('groups', 'seq', 'row'), None, 'col'), may hold values from -24 to 24
- out_weight: bfloat16 [1024, 128], replicated, may hold values from -0.1875 to 0.1875
- out_bias: float32 [128], replicated, may hold values from -6 to 6
- chain_lengths: int32 [12], P('groups'), may hold values from 1 to 128, 512 in all
- unpaired_depths: int32 [12], P('groups'), may hold values from 256 to 1024
Outputs:
- pair_update: bfloat16 [512, 512, 128], P(('groups', 'row'), ('col', 'seq'))
Inputs may be any that keep to these rules, and one draw needn't show every extreme that they name: `chain_lengths`: chain lengths sum to 512. `unpaired_depths`: rows of the unpaired MSA at or beyond a chain's depth are padding.
All inputs are finite; a program needn't handle non-finite values.
Results may differ from a plain program's by a relative error of at most 0.0034.
Values may be sent and summed in bfloat16 or wider, within the bound.
A program may use at most 128 MiB of HBM per device.

v0:
```python
import jax
import jax.numpy as jnp
from jax import lax
from jax.sharding import PartitionSpec as P

CHAINS = 12
S_P = 512


def body(
    paired_left,
    paired_right,
    unpaired_left,
    unpaired_right,
    out_weight,
    out_bias,
    chain_lengths,
    unpaired_depths,
):
    left_pair, left_free = (
        lax.all_gather(paired_left, "col", axis=0, tiled=True),
        lax.all_gather(unpaired_left, "col", axis=0, tiled=True),
    )
    right_pair, right_free = (
        lax.all_gather(paired_right, "row", axis=0, tiled=True),
        lax.all_gather(unpaired_right, "row", axis=0, tiled=True),
    )
    rows_here = left_pair.shape[2]
    cols_here = right_pair.shape[2]
    first_row = lax.axis_index("row") * rows_here
    first_col = lax.axis_index("col") * cols_here
    residues = rows_here * lax.axis_size("row")
    positions = jnp.arange(residues, dtype=jnp.int32)
    chain_ends = jnp.cumsum(chain_lengths)
    chain_of = jnp.sum((positions[:, None] >= chain_ends[None, :]).astype(jnp.int32), axis=1)
    onehot = chain_of[:, None] == jnp.arange(CHAINS, dtype=jnp.int32)[None, :]
    depth_of = jnp.sum(jnp.where(onehot, unpaired_depths[None, :], 0), axis=1)
    chain_rows = lax.dynamic_slice_in_dim(chain_of, first_row, rows_here, 0)
    depth_rows = lax.dynamic_slice_in_dim(depth_of, first_row, rows_here, 0)
    chain_cols = lax.dynamic_slice_in_dim(chain_of, first_col, cols_here, 0)
    free_count = left_free.shape[0]
    free_ids = lax.axis_index("seq") * free_count + jnp.arange(free_count, dtype=jnp.int32)
    live_rows = (free_ids[:, None] < depth_rows[None, :]).astype(left_free.dtype)
    left_free = left_free * live_rows[:, None, :]
    same_chain = (chain_rows[:, None] == chain_cols[None, :]).astype(jnp.float32)
    block_rows = 4
    channels = out_weight.shape[1]

    def one_block(block_index):
        offset = block_index * block_rows
        left_block = lax.dynamic_slice_in_dim(left_pair, offset, block_rows, 2)
        free_block = lax.dynamic_slice_in_dim(left_free, offset, block_rows, 2)
        same_block = lax.dynamic_slice_in_dim(same_chain, offset, block_rows, 0)
        paired = jnp.einsum(
            "sci,sdj->ijcd", left_block, right_pair, preferred_element_type=jnp.float32
        )
        unpaired = jnp.einsum(
            "sci,sdj->ijcd", free_block, right_free, preferred_element_type=jnp.float32
        )
        unpaired = unpaired * same_block[:, :, None, None]
        outer_product = (paired + unpaired).astype(jnp.bfloat16).reshape(block_rows * cols_here, -1)
        projected = jnp.dot(outer_product, out_weight, preferred_element_type=jnp.float32)
        return projected.reshape(block_rows, cols_here, channels)

    projected = lax.map(one_block, jnp.arange(rows_here // block_rows, dtype=jnp.int32))
    projected = projected.reshape(rows_here, cols_here, channels)
    half_cols = cols_here // lax.axis_size("seq")
    own_offset = lax.axis_index("seq") * half_cols
    summed = lax.psum(projected, "seq")
    own_share = lax.dynamic_slice_in_dim(summed, own_offset, half_cols, 1)
    same_share = lax.dynamic_slice_in_dim(same_chain, own_offset, half_cols, 1)
    denominator = S_P + same_share * depth_rows[:, None].astype(jnp.float32)
    return (own_share / denominator[:, :, None] + out_bias).astype(jnp.bfloat16)


def solution(mesh):
    return jax.shard_map(
        body,
        mesh=mesh,
        in_specs=(
            P(("groups", "seq", "col"), None, "row"),
            P(("groups", "seq", "row"), None, "col"),
            P(("groups", "seq", "col"), None, "row"),
            P(("groups", "seq", "row"), None, "col"),
            P(),
            P(),
            P("groups"),
            P("groups"),
        ),
        out_specs=P(("groups", "row"), ("col", "seq"), None),
        check_vma=False,
    )
```

profile of v0, /device:TPU:5, one launch (start us, length us, event | category | flops | bytes accessed | tf_op | source)
XLA Modules:
  0.0 416.1 jit_solution(13821288054562423677)
XLA Ops:
  6.5 2.9 copy.23
  9.5 2.2 copy.21
  15.4 28.3 %all-gather.9.cloned.1.call-done = bf16[1024,32,32]{0,1,2:T(8,128)(2,1)} async-done(((bf16[512,32,32]{0,1,2:T(8,128)(2,1)}), bf16[1024,32,32]{0,1,2:T(8,128)(2,1)}) %all-gather.9.cloned.1.call-update) | async-done | bytes 2097168 | tf_op jit(solution)/shard_map/all_gather | solution.py:22
  45.5 21.1 %all-gather.5.cloned.1.call-done = bf16[512,32,32]{0,1,2:T(8,128)(2,1)} async-done(((bf16[256,32,32]{0,1,2:T(8,128)(2,1)}), bf16[512,32,32]{0,1,2:T(8,128)(2,1)}) %all-gather.5.cloned.1.call-update) | async-done | bytes 1048592 | tf_op jit(solution)/shard_map/all_gather | solution.py:21
  66.6 76.2 %all-gather.7.cloned.1.call-done = bf16[512,32,256]{2,0,1:T(8,128)(2,1)} async-done(((bf16[32,32,256]{2,0,1:T(8,128)(2,1)}), bf16[512,32,256]{2,0,1:T(8,128)(2,1)}) %all-gather.7.cloned.1.call-update) | async-done | bytes 8388624 | tf_op jit(solution)/shard_map/all_gather | solution.py:25
  142.8 127.1 %all-gather.11.cloned.1.call-done = bf16[1024,32,256]{2,0,1:T(8,128)(2,1)} async-done(((bf16[64,32,256]{2,0,1:T(8,128)(2,1)}), bf16[1024,32,256]{2,0,1:T(8,128)(2,1)}) %all-gather.11.cloned.1.call-update) | async-done | bytes 16777232 | tf_op jit(solution)/shard_map/all_gather | solution.py:26
  269.9 135.9 %while.10 = (s32[]{:T(128)}, f32[8,4,256,128]{3,2,1,0:T(8,128)}, s32[8]{0:T(128)S(1)}, bf16[512,32,32]{0,1,2:T(8,128)(2,1)}, bf16[512,32,256]{2,0,1:T(8,128)(2,1...) while((s32[]{:T(128)}, f32[8,4,256,128]{3,2,1,0:T(8,128)}, ...), condition=%wide.region_4.5_spmd, body=%wide.region_3.4_spmd.sunk | while | flops 3492806656 | bytes 43135680 | solution.py:65
  271.1 4.7 %fusion.36 = f32[32,4,32,256]{3,0,2,1:T(8,128)S(1)} fusion(bf16[512,32,256]{2,0,1:T(8,128)(2,1)} %get-tuple-element.158, bf16[512,32,32]{0,1,2:T(8,128)(2,1)} %get-tuple-element.157, s32[]{:T(128)S(6)} %select_n.23), kind=kOutput, calls=%fused_computation.2.clone.1 | convolution fusion | flops 1073741824 | bytes 12713988 | tf_op jit(solution)/shard_map/while/body/eval_jaxpr/sci,sdj->ijcd/dot_general | solution.py:54
  275.9 8.2 %fusion.37 = bf16[4,256,32,32]{1,2,3,0:T(8,128)(2,1)S(1)} fusion(f32[32,4,32,256]{3,0,2,1:T(8,128)S(1)} %fusion.36, f32[4,256]{1,0:T(4,128)S(1)} %constant_dynamic-slice_fusion.2, bf16[1024,32,256]{2,0,1:T(8,128)(2,1)} %get-tuple-element.160, bf16[1024,32,32]{0,1,2:T(8,128)(2,1)S(1)} %get-tuple-element.159, s32[]{:T(128)S(6)} %select_n.23), kind=kOutput, calls=%fused_computation.5.clone.1 | convolution fusion | flops 2150629376 | bytes 23334916 | tf_op jit(solution)/shard_map/while/body/eval_jaxpr/sci,sdj->ijcd/dot_general | solution.py:57
  288.1 4.7 %fusion.36 = f32[32,4,32,256]{3,0,2,1:T(8,128)S(1)} fusion(bf16[512,32,256]{2,0,1:T(8,128)(2,1)} %get-tuple-element.158, bf16[512,32,32]{0,1,2:T(8,128)(2,1)} %get-tuple-element.157, s32[]{:T(128)S(6)} %select_n.23), kind=kOutput, calls=%fused_computation.2.clone.1 | convolution fusion | flops 1073741824 | bytes 12713988 | tf_op jit(solution)/shard_map/while/body/eval_jaxpr/sci,sdj->ijcd/dot_general | solution.py:54
  292.9 8.2 %fusion.37 = bf16[4,256,32,32]{1,2,3,0:T(8,128)(2,1)S(1)} fusion(f32[32,4,32,256]{3,0,2,1:T(8,128)S(1)} %fusion.36, f32[4,256]{1,0:T(4,128)S(1)} %constant_dynamic-slice_fusion.2, bf16[1024,32,256]{2,0,1:T(8,128)(2,1)} %get-tuple-element.160, bf16[1024,32,32]{0,1,2:T(8,128)(2,1)S(1)} %get-tuple-element.159, s32[]{:T(128)S(6)} %select_n.23), kind=kOutput, calls=%fused_computation.5.clone.1 | convolution fusion | flops 2150629376 | bytes 23334916 | tf_op jit(solution)/shard_map/while/body/eval_jaxpr/sci,sdj->ijcd/dot_general | solution.py:57
  305.1 4.7 %fusion.36 = f32[32,4,32,256]{3,0,2,1:T(8,128)S(1)} fusion(bf16[512,32,256]{2,0,1:T(8,128)(2,1)} %get-tuple-element.158, bf16[512,32,32]{0,1,2:T(8,128)(2,1)} %get-tuple-element.157, s32[]{:T(128)S(6)} %select_n.23), kind=kOutput, calls=%fused_computation.2.clone.1 | convolution fusion | flops 1073741824 | bytes 12713988 | tf_op jit(solution)/shard_map/while/body/eval_jaxpr/sci,sdj->ijcd/dot_general | solution.py:54
  309.9 8.2 %fusion.37 = bf16[4,256,32,32]{1,2,3,0:T(8,128)(2,1)S(1)} fusion(f32[32,4,32,256]{3,0,2,1:T(8,128)S(1)} %fusion.36, f32[4,256]{1,0:T(4,128)S(1)} %constant_dynamic-slice_fusion.2, bf16[1024,32,256]{2,0,1:T(8,128)(2,1)} %get-tuple-element.160, bf16[1024,32,32]{0,1,2:T(8,128)(2,1)S(1)} %get-tuple-element.159, s32[]{:T(128)S(6)} %select_n.23), kind=kOutput, calls=%fused_computation.5.clone.1 | convolution fusion | flops 2150629376 | bytes 23334916 | tf_op jit(solution)/shard_map/while/body/eval_jaxpr/sci,sdj->ijcd/dot_general | solution.py:57
  322.1 4.7 %fusion.36 = f32[32,4,32,256]{3,0,2,1:T(8,128)S(1)} fusion(bf16[512,32,256]{2,0,1:T(8,128)(2,1)} %get-tuple-element.158, bf16[512,32,32]{0,1,2:T(8,128)(2,1)} %get-tuple-element.157, s32[]{:T(128)S(6)} %select_n.23), kind=kOutput, calls=%fused_computation.2.clone.1 | convolution fusion | flops 1073741824 | bytes 12713988 | tf_op jit(solution)/shard_map/while/body/eval_jaxpr/sci,sdj->ijcd/dot_general | solution.py:54
  326.9 8.2 %fusion.37 = bf16[4,256,32,32]{1,2,3,0:T(8,128)(2,1)S(1)} fusion(f32[32,4,32,256]{3,0,2,1:T(8,128)S(1)} %fusion.36, f32[4,256]{1,0:T(4,128)S(1)} %constant_dynamic-slice_fusion.2, bf16[1024,32,256]{2,0,1:T(8,128)(2,1)} %get-tuple-element.160, bf16[1024,32,32]{0,1,2:T(8,128)(2,1)S(1)} %get-tuple-element.159, s32[]{:T(128)S(6)} %select_n.23), kind=kOutput, calls=%fused_computation.5.clone.1 | convolution fusion | flops 2150629376 | bytes 23334916 | tf_op jit(solution)/shard_map/while/body/eval_jaxpr/sci,sdj->ijcd/dot_general | solution.py:57
  339.1 4.7 %fusion.36 = f32[32,4,32,256]{3,0,2,1:T(8,128)S(1)} fusion(bf16[512,32,256]{2,0,1:T(8,128)(2,1)} %get-tuple-element.158, bf16[512,32,32]{0,1,2:T(8,128)(2,1)} %get-tuple-element.157, s32[]{:T(128)S(6)} %select_n.23), kind=kOutput, calls=%fused_computation.2.clone.1 | convolution fusion | flops 1073741824 | bytes 12713988 | tf_op jit(solution)/shard_map/while/body/eval_jaxpr/sci,sdj->ijcd/dot_general | solution.py:54
  343.8 8.2 %fusion.37 = bf16[4,256,32,32]{1,2,3,0:T(8,128)(2,1)S(1)} fusion(f32[32,4,32,256]{3,0,2,1:T(8,128)S(1)} %fusion.36, f32[4,256]{1,0:T(4,128)S(1)} %constant_dynamic-slice_fusion.2, bf16[1024,32,256]{2,0,1:T(8,128)(2,1)} %get-tuple-element.160, bf16[1024,32,32]{0,1,2:T(8,128)(2,1)S(1)} %get-tuple-element.159, s32[]{:T(128)S(6)} %select_n.23), kind=kOutput, calls=%fused_computation.5.clone.1 | convolution fusion | flops 2150629376 | bytes 23334916 | tf_op jit(solution)/shard_map/while/body/eval_jaxpr/sci,sdj->ijcd/dot_general | solution.py:57
  356.1 4.7 %fusion.36 = f32[32,4,32,256]{3,0,2,1:T(8,128)S(1)} fusion(bf16[512,32,256]{2,0,1:T(8,128)(2,1)} %get-tuple-element.158, bf16[512,32,32]{0,1,2:T(8,128)(2,1)} %get-tuple-element.157, s32[]{:T(128)S(6)} %select_n.23), kind=kOutput, calls=%fused_computation.2.clone.1 | convolution fusion | flops 1073741824 | bytes 12713988 | tf_op jit(solution)/shard_map/while/body/eval_jaxpr/sci,sdj->ijcd/dot_general | solution.py:54
  360.8 8.2 %fusion.37 = bf16[4,256,32,32]{1,2,3,0:T(8,128)(2,1)S(1)} fusion(f32[32,4,32,256]{3,0,2,1:T(8,128)S(1)} %fusion.36, f32[4,256]{1,0:T(4,128)S(1)} %constant_dynamic-slice_fusion.2, bf16[1024,32,256]{2,0,1:T(8,128)(2,1)} %get-tuple-element.160, bf16[1024,32,32]{0,1,2:T(8,128)(2,1)S(1)} %get-tuple-element.159, s32[]{:T(128)S(6)} %select_n.23), kind=kOutput, calls=%fused_computation.5.clone.1 | convolution fusion | flops 2150629376 | bytes 23334916 | tf_op jit(solution)/shard_map/while/body/eval_jaxpr/sci,sdj->ijcd/dot_general | solution.py:57
  373.0 4.7 %fusion.36 = f32[32,4,32,256]{3,0,2,1:T(8,128)S(1)} fusion(bf16[512,32,256]{2,0,1:T(8,128)(2,1)} %get-tuple-element.158, bf16[512,32,32]{0,1,2:T(8,128)(2,1)} %get-tuple-element.157, s32[]{:T(128)S(6)} %select_n.23), kind=kOutput, calls=%fused_computation.2.clone.1 | convolution fusion | flops 1073741824 | bytes 12713988 | tf_op jit(solution)/shard_map/while/body/eval_jaxpr/sci,sdj->ijcd/dot_general | solution.py:54
  377.8 8.2 %fusion.37 = bf16[4,256,32,32]{1,2,3,0:T(8,128)(2,1)S(1)} fusion(f32[32,4,32,256]{3,0,2,1:T(8,128)S(1)} %fusion.36, f32[4,256]{1,0:T(4,128)S(1)} %constant_dynamic-slice_fusion.2, bf16[1024,32,256]{2,0,1:T(8,128)(2,1)} %get-tuple-element.160, bf16[1024,32,32]{0,1,2:T(8,128)(2,1)S(1)} %get-tuple-element.159, s32[]{:T(128)S(6)} %select_n.23), kind=kOutput, calls=%fused_computation.5.clone.1 | convolution fusion | flops 2150629376 | bytes 23334916 | tf_op jit(solution)/shard_map/while/body/eval_jaxpr/sci,sdj->ijcd/dot_general | solution.py:57
  390.0 4.7 %fusion.36 = f32[32,4,32,256]{3,0,2,1:T(8,128)S(1)} fusion(bf16[512,32,256]{2,0,1:T(8,128)(2,1)} %get-tuple-element.158, bf16[512,32,32]{0,1,2:T(8,128)(2,1)} %get-tuple-element.157, s32[]{:T(128)S(6)} %select_n.23), kind=kOutput, calls=%fused_computation.2.clone.1 | convolution fusion | flops 1073741824 | bytes 12713988 | tf_op jit(solution)/shard_map/while/body/eval_jaxpr/sci,sdj->ijcd/dot_general | solution.py:54
  394.8 8.2 %fusion.37 = bf16[4,256,32,32]{1,2,3,0:T(8,128)(2,1)S(1)} fusion(f32[32,4,32,256]{3,0,2,1:T(8,128)S(1)} %fusion.36, f32[4,256]{1,0:T(4,128)S(1)} %constant_dynamic-slice_fusion.2, bf16[1024,32,256]{2,0,1:T(8,128)(2,1)} %get-tuple-element.160, bf16[1024,32,32]{0,1,2:T(8,128)(2,1)S(1)} %get-tuple-element.159, s32[]{:T(128)S(6)} %select_n.23), kind=kOutput, calls=%fused_computation.5.clone.1 | convolution fusion | flops 2150629376 | bytes 23334916 | tf_op jit(solution)/shard_map/while/body/eval_jaxpr/sci,sdj->ijcd/dot_general | solution.py:57
  405.8 3.8 fusion.16
  (66 shorter events, 32.3 us)
Async XLA Ops:
  6.5 5.2 %copy-start.2 = (bf16[32,32,256]{2,1,0:T(8,128)(2,1)S(1)}, bf16[32,32,256]{2,1,0:T(8,128)(2,1)}, u32[]{:S(2)}) copy-start(bf16[32,32,256]{2,1,0:T(8,128)(2,1)} %param.11) | copy-start | bytes 1572868
  6.5 6.4 %copy-start.1 = (bf16[64,32,256]{2,1,0:T(8,128)(2,1)S(1)}, bf16[64,32,256]{2,1,0:T(8,128)(2,1)}, u32[]{:S(2)}) copy-start(bf16[64,32,256]{2,1,0:T(8,128)(2,1)} %param.13) | copy-start | bytes 3145732
  6.5 37.2 %all-gather.9.cloned.1.call-start = ((), (), s32[]{:S(2)}) async-start(), calls=%async_computation.2 | async-start | bytes 3145728 | tf_op jit(solution)/shard_map/all_gather | solution.py:22
  9.4 5.1 %copy-start.5 = (s32[12]{0:T(128)S(1)}, s32[12]{0:T(128)}, u32[]{:S(2)}) copy-start(s32[12]{0:T(128)} %param.16) | copy-start | bytes 148
  9.4 5.6 %copy-start.4 = (s32[12]{0:T(128)S(1)}, s32[12]{0:T(128)}, u32[]{:S(2)}) copy-start(s32[12]{0:T(128)} %param.17) | copy-start | bytes 148
  9.5 57.1 %all-gather.5.cloned.1.call-start = ((), (), s32[]{:S(2)}) async-start(), calls=%async_computation | async-start | bytes 1572864 | tf_op jit(solution)/shard_map/all_gather | solution.py:21
  11.7 131.1 %all-gather.7.cloned.1.call-start = ((), (), s32[]{:S(2)}) async-start(), calls=%async_computation.1 | async-start | bytes 8912896 | tf_op jit(solution)/shard_map/all_gather | solution.py:25
  12.9 257.0 %copy-start = (bf16[1024,128]{1,0:T(8,128)(2,1)S(1)}, bf16[1024,128]{1,0:T(8,128)(2,1)}, u32[]{:S(2)}) copy-start(bf16[1024,128]{1,0:T(8,128)(2,1)} %param.14) | copy-start | bytes 786436
  12.9 257.0 %all-gather.11.cloned.1.call-start = ((), (), s32[]{:S(2)}) async-start(), calls=%async_computation.3 | async-start | bytes 17825792 | tf_op jit(solution)/shard_map/all_gather | solution.py:26
  269.9 135.9 %copy-start.3 = (f32[128]{0:T(128)S(1)}, f32[128]{0:T(128)}, u32[]{:S(2)}) copy-start(f32[128]{0:T(128)} %param.15) | copy-start | bytes 1540
Sparse Core Ops, SparseCore 0:
  9.6 34.1 all-gather.8
  45.3 21.2 all-gather.4
  68.7 73.9 all-gather.6
  144.8 125.0 all-gather.10
where the time goes:
time: 419 us; the launch traced here: 416 us
  waiting for transfers between devices  253 us (60%)
  matrix products  116 us (28%)
  local copies, waits for them, and re-layouts  22.2 us (5%)
  between operations  13.2 us (3%)
  other arithmetic  6.23 us (1%)
  loops' own time  5.49 us (1%)
    all_gather x1, waiting for transfers between devices, body(): lax.all_gather(unpaired_right, 'row', axis=0, tiled=True)  127 us
    all_gather x1, waiting for transfers between devices, body(): lax.all_gather(paired_right, 'row', axis=0, tiled=True)  76.2 us
    dot_general x8, matrix products, one_block(): jnp.einsum('sci,sdj->ijcd', free_block, right_free, preferred_element_typ...  65.7 us
    dot_general x8, matrix products, one_block(): jnp.einsum('sci,sdj->ijcd', left_block, right_pair, preferred_element_typ...  37.9 us
    all_gather x1, waiting for transfers between devices, body(): lax.all_gather(unpaired_left, 'col', axis=0, tiled=True)  28.3 us
    all_gather x1, waiting for transfers between devices, body(): lax.all_gather(paired_left, 'col', axis=0, tiled=True)  21.1 us
    dot_general x8, matrix products, one_block(): jnp.dot(outer_product, out_weight, preferred_element_type=jnp.float32)  12.6 us
    convert_element_type x8, local copies, waits for them, and re-layouts, one_block(): (paired + unpaired).astype(jnp.bfloat16).reshape(block_rows * cols_here, -1)  9.51 us
  transfers between devices with their start and end apart: 4, of which 4 were waited for; matrix products, arithmetic and copies ran while one was open for 2% of the time, Pallas kernels for 0%

commit v1 on v0

v1 whole, which is shorter than its diff:
```python
import functools

import jax
import jax.numpy as jnp
from jax import lax
from jax.experimental import pallas as pl
from jax.experimental.pallas import tpu as pltpu
from jax.sharding import PartitionSpec as P

LANES = 128
D_STEP = 8


def outer_kernel(
    paired_total, group, final,
    start_ref, end_ref, depth_ref,
    left_pair, left_free, right_pair, right_free, weight, bias,
    out_ref, outer_scr, free_scr, acc,
):
    tile, step = pl.program_id(0), pl.program_id(1)
    rows = start_ref.shape[0]
    channels = left_pair.shape[0] // rows
    width = right_pair.shape[1]
    d_step = width // LANES
    lanes = lax.broadcasted_iota(jnp.int32, (1, LANES), 1) + tile * LANES
    span = group * channels

    @pl.loop(0, rows // group)
    def _(g):
        base = g * group
        at = pl.ds(pl.multiple_of(base * channels, span), span)
        outer_scr[...] = jnp.dot(left_pair[at, :], right_pair[...], preferred_element_type=jnp.float32)
        first, last = start_ref[base], end_ref[base + group - 1]

        @pl.when((first < (tile + 1) * LANES) & (last > tile * LANES))
        def _():
            free_scr[...] = jnp.dot(left_free[at, :], right_free[...], preferred_element_type=jnp.float32)
            for i in range(group):
                same = (lanes >= start_ref[base + i]) & (lanes < end_ref[base + i])
                part = pl.ds(i * channels, channels)
                for d in range(d_step):
                    cols = pl.ds(d * LANES, LANES)
                    outer_scr[part, cols] += jnp.where(same, free_scr[part, cols], 0.0)

        for pair in range(group // 2):
            halves = []
            for i in (2 * pair, 2 * pair + 1):
                mine = outer_scr[pl.ds(i * channels, channels), :].astype(jnp.bfloat16)
                halves.append(jnp.concatenate(
                    [mine[:, d * LANES:(d + 1) * LANES] for d in range(d_step)], axis=0))
            projected = jnp.dot(
                weight[...], jnp.concatenate(halves, axis=1), preferred_element_type=jnp.float32)
            for k in range(2):
                row = base + 2 * pair + k
                value = projected[:, k * LANES:(k + 1) * LANES]

                @pl.when(step == 0)
                def _():
                    acc[row] = value

                @pl.when(step > 0)
                def _():
                    acc[row] += value

    @pl.when(step == pl.num_programs(1) - 1)
    def _():
        @pl.loop(0, rows)
        def _(i):
            same = (lanes >= start_ref[i]) & (lanes < end_ref[i])
            depth = depth_ref[i].astype(jnp.float32)
            count = paired_total + jnp.where(same, depth, 0.0)
            value = (acc[i] / count).T
            if final:
                value = value + bias[...]
            out_ref[i] = value.astype(out_ref.dtype)


def outer_product(left_pair, left_free, right_pair, right_free, weight, bias, start, end, depth, paired_total, final):
    rows = start.shape[0]
    channels = left_pair.shape[0] // rows
    out_channels = weight.shape[0]
    cols = right_pair.shape[1] // channels
    group = min(16, rows)
    width = D_STEP * LANES
    steps = channels // D_STEP
    smem = pl.BlockSpec(memory_space=pltpu.SMEM)

    def whole(x):
        return pl.BlockSpec(x.shape, lambda t, s: (0, 0))

    def streamed(x):
        return pl.BlockSpec((x.shape[0], width), lambda t, s: (0, t * steps + s))

    return pl.pallas_call(
        functools.partial(outer_kernel, float(paired_total), group, final),
        out_shape=jax.ShapeDtypeStruct((rows, cols, out_channels), jnp.bfloat16 if final else jnp.float32),
        grid=(cols // LANES, steps),
        in_specs=[
            smem, smem, smem, whole(left_pair), whole(left_free), streamed(right_pair), streamed(right_free),
            pl.BlockSpec((out_channels, D_STEP * channels), lambda t, s: (0, s)), whole(bias),
        ],
        out_specs=pl.BlockSpec((rows, LANES, out_channels), lambda t, s: (0, t, 0)),
        scratch_shapes=[
            pltpu.VMEM((group * channels, width), jnp.float32),
            pltpu.VMEM((group * channels, width), jnp.float32),
            pltpu.VMEM((rows, out_channels, LANES), jnp.float32),
        ],
        compiler_params=pltpu.CompilerParams(
            dimension_semantics=("arbitrary", "arbitrary"), vmem_limit_bytes=56 << 20),
        name="outer_product",
    )(start, end, depth, left_pair, left_free, right_pair, right_free, weight, bias)


def flat_right(x):
    depth, channels, cols = x.shape
    return x.reshape(depth, channels, cols // LANES, LANES).transpose(0, 2, 1, 3).reshape(depth, -1)


def flat_left(x):
    depth, channels, rows = x.shape
    return x.transpose(2, 1, 0).reshape(rows * channels, depth)


def body(
    paired_left, paired_right, unpaired_left, unpaired_right,
    out_weight, out_bias, chain_lengths, unpaired_depths,
):
    channels, rows = paired_left.shape[1:]
    cols = paired_right.shape[2]
    first_row = lax.axis_index("row") * rows
    first_col = lax.axis_index("col") * cols
    positions = first_row + jnp.arange(rows, dtype=jnp.int32)
    chain_ends = jnp.cumsum(chain_lengths)
    chain_starts = chain_ends - chain_lengths
    inside = (positions[:, None] >= chain_starts[None, :]) & (positions[:, None] < chain_ends[None, :])

    def pick(table):
        return jnp.sum(jnp.where(inside, table[None, :], 0), axis=1, dtype=jnp.int32)

    depth = pick(unpaired_depths)
    start = pick(chain_starts) - first_col
    end = pick(chain_ends) - first_col

    seq = lax.axis_size("seq")
    free_here = unpaired_left.shape[0]
    first_free = (lax.axis_index("seq") * lax.axis_size("col") + lax.axis_index("col")) * free_here
    free_ids = first_free + jnp.arange(free_here, dtype=jnp.int32)
    live = free_ids[:, None] < depth[None, :]
    masked = jnp.where(live[:, None, :], unpaired_left, jnp.zeros((), unpaired_left.dtype))

    right_pair = lax.all_gather(flat_right(paired_right), "row", axis=0, tiled=True)
    right_free = lax.all_gather(flat_right(unpaired_right), "row", axis=0, tiled=True)
    left_pair = lax.all_gather(flat_left(paired_left), "col", axis=1, tiled=True)
    left_free = lax.all_gather(flat_left(masked), "col", axis=1, tiled=True)

    out_channels = out_weight.shape[1]
    weight = out_weight.reshape(channels, channels, out_channels).transpose(2, 1, 0).reshape(out_channels, -1)
    bias = out_bias.reshape(1, -1)
    paired_total = right_pair.shape[0] * seq
    out = outer_product(
        left_pair, left_free, right_pair, right_free, weight, bias, start, end, depth, paired_total, seq == 1)
    if seq == 1:
        return out
    summed = lax.psum(out, "seq")
    share = cols // seq
    own = lax.dynamic_slice_in_dim(summed, lax.axis_index("seq") * share, share, 1)
    return (own + bias).astype(jnp.bfloat16)


def solution(mesh):
    return jax.shard_map(
        body,
        mesh=mesh,
        in_specs=(
            P(("groups", "seq", "col"), None, "row"),
            P(("groups", "seq", "row"), None, "col"),
            P(("groups", "seq", "col"), None, "row"),
            P(("groups", "seq", "row"), None, "col"),
            P(),
            P(),
            P("groups"),
            P("groups"),
        ),
        out_specs=P(("groups", "row"), ("col", "seq"), None),
        check_vma=False,
    )
```

time: 419 us -> 344 us (0.82)
  matrix products: 116 us -> 0 us
  Pallas kernels: 0 us -> 63.5 us
  local copies, waits for them, and re-layouts: 22.2 us -> 8.97 us
  loops' own time: 5.49 us -> 0 us
    dot_general x24 -> x0, matrix products: 116 us -> none  [the longest x8 65.7 us: one_block(): jnp.einsum('sci,sdj->ijcd', free_block, right_free, preferred_element_typ...]
    pallas_call x0 -> x1, Pallas kernels: none -> 63.5 us  [outer_product(): pl.pallas_call(functools.partial(outer_kernel, float(paired_total), group...]
    convert_element_type x8 -> x0, local copies, waits for them, and re-layouts: 9.51 us -> none  [one_block(): (paired + unpaired).astype(jnp.bfloat16).reshape(block_rows * cols_here, -1)]
    another operation x1 -> x0, loops' own time: 5.49 us -> none  [body(): lax.map(one_block, jnp.arange(rows_here // block_rows, dtype=jnp.int32))]
    dynamic_slice x18 -> x0, local copies, waits for them, and re-layouts: 4.9 us -> none  [the longest x8 4.66 us: body(): lax.map(one_block, jnp.arange(rows_here // block_rows, dtype=jnp.int32))]
    unnamed x16 -> x8, local copies, waits for them, and re-layouts: 7.75 us -> 2.88 us
  transfers between devices with their start and end apart: 4 -> 4, of which waited for: 4 -> 4; matrix products, arithmetic and copies ran while one was open for 2% -> 3% of each run, Pallas kernels for 0% -> 0%
where the time goes in v1:
time: 344 us; the launch traced here: 339 us
  waiting for transfers between devices  249 us (72%)
  Pallas kernels  63.5 us (18%)
  between operations  13.2 us (4%)
  local copies, waits for them, and re-layouts  8.97 us (3%)
  other arithmetic  4.21 us (1%)
    all_gather x1, waiting for transfers between devices, body(): lax.all_gather(flat_right(unpaired_right), 'row', axis=0, tiled=True)  127 us
    all_gather x1, waiting for transfers between devices, body(): lax.all_gather(flat_right(paired_right), 'row', axis=0, tiled=True)  76.2 us
    pallas_call x1, Pallas kernels, outer_product(): pl.pallas_call(functools.partial(outer_kernel, float(paired_total), group...  63.5 us
    all_gather x1, waiting for transfers between devices, body(): left_free = lax.all_gather(flat_left(masked), 'col', axis=1, tiled=True)  34.7 us
    all_gather x1, waiting for transfers between devices, body(): lax.all_gather(flat_left(paired_left), 'col', axis=1, tiled=True)  11.3 us
  transfers between devices with their start and end apart: 4, of which 4 were waited for; matrix products, arithmetic and copies ran while one was open for 3% of the time, Pallas kernels for 0%

profile of v1, /device:TPU:5, one launch (start us, length us, event | category | flops | bytes accessed | tf_op | source)
XLA Modules:
  0.0 339.2 jit_solution(7954130679203385476)
XLA Ops:
  6.5 2.3 copy.25
  8.8 0.0 all-gather.5.cloned.1.call-update
  8.8 0.0 all-gather.7.cloned.1.call-start
  8.9 0.8 reduce-window.8
  9.7 0.7 bitcast_subtract_fusion
  10.4 0.7 select_reduce_fusion
  11.1 0.1 broadcast_compare_fusion
  11.2 1.3 select_bitcast_fusion
  12.5 1.5 copy.26
  14.1 0.0 all-gather.7.cloned.1.call-update
  14.1 0.0 all-gather.9.cloned.1.call-start
  14.1 1.1 copy_bitcast_fusion.3
  15.3 1.2 copy.40
  16.5 0.0 all-gather.11.cloned.1.call-start
  16.5 0.2 copy_bitcast_fusion.1
  16.7 1.7 copy.39
  18.5 0.1 copy.29
  18.6 0.8 copy.30.weight
  19.4 0.6 broadcast_subtract_fusion
  20.0 11.3 %all-gather.5.cloned.1.call-done.left_pair = bf16[1024,512]{1,0:T(8,128)(2,1)} async-done(((bf16[1024,256]{1,0:T(8,128)(2,1)}), bf16[1024,512]{1,0:T(8,128)(2,1)}) %all-gather.5.cloned.1.call-update) | async-done | bytes 1048592 | tf_op jit(solution)/shard_map/all_gather | solution.py:153
  31.3 34.7 %all-gather.7.cloned.1.call-done.left_free = bf16[1024,1024]{1,0:T(8,128)(2,1)} async-done(((bf16[1024,512]{1,0:T(8,128)(2,1)}), bf16[1024,1024]{1,0:T(8,128)(2,1)}) %all-gather.7.cloned.1.call-update) | async-done | bytes 2097168 | tf_op jit(solution)/shard_map/all_gather | solution.py:154
  66.0 76.2 %all-gather.9.cloned.1.call-done.right_pair = bf16[512,8192]{1,0:T(8,128)(2,1)} async-done(((bf16[32,8192]{1,0:T(8,128)(2,1)}), bf16[512,8192]{1,0:T(8,128)(2,1)}) %all-gather.9.cloned.1.call-update) | async-done | bytes 8388624 | tf_op jit(solution)/shard_map/all_gather | solution.py:151
  142.1 127.1 %all-gather.11.cloned.1.call-done.right_free = bf16[1024,8192]{1,0:T(8,128)(2,1)} async-done(((bf16[64,8192]{1,0:T(8,128)(2,1)}), bf16[1024,8192]{1,0:T(8,128)(2,1)}) %all-gather.11.cloned.1.call-update) | async-done | bytes 16777232 | tf_op jit(solution)/shard_map/all_gather | solution.py:152
  269.2 63.5 %outer_product.1 = bf16[32,256,128]{2,1,0:T(8,128)(2,1)} custom-call(s32[32]{0:T(128)} %get-tuple-element.9.start_ref, s32[32]{0:T(128)} %get-tuple-element.8.end_ref, s32[32]{0:T(128)} %copy-done.2, bf16[1024,512]{1,0:T(8,128)(2,1)} %all-gather.5.cloned.1.call-done.left_pair, bf16[1024,1024]{1,0:T(8,128)(2,1)} %all-gather.7.cloned.1.call-done.left_free, ...), custom_call_target="tpu_custom_call" | custom-call | tf_op jit(solution)/shard_map/outer_product/pallas_call | solution.py:94
  (11 shorter events, 0.1 us)
Async XLA Ops:
  6.5 10.0 %copy-start = (bf16[64,32,256]{2,1,0:T(8,128)(2,1)S(1)}, bf16[64,32,256]{2,1,0:T(8,128)(2,1)}, u32[]{:S(2)}) copy-start(bf16[64,32,256]{2,1,0:T(8,128)(2,1)} %param.11) | copy-start | bytes 3145732
  6.5 11.9 %copy-start.1 = (bf16[1024,128]{1,0:T(8,128)(2,1)S(1)}, bf16[1024,128]{1,0:T(8,128)(2,1)}, u32[]{:S(2)}) copy-start(bf16[1024,128]{1,0:T(8,128)(2,1)} %param.12) | copy-start | bytes 786436
  6.5 24.8 %all-gather.5.cloned.1.call-start = ((), (), s32[]{:S(2)}) async-start(), calls=%async_computation | async-start | bytes 1572864 | tf_op jit(solution)/shard_map/all_gather | solution.py:153
  8.8 57.1 %all-gather.7.cloned.1.call-start = ((), (), s32[]{:S(2)}) async-start(), calls=%async_computation.1 | async-start | bytes 3145728 | tf_op jit(solution)/shard_map/all_gather | solution.py:154
  11.1 258.1 %copy-start.2 = (s32[32]{0:T(128)}, s32[32]{0:T(128)S(1)}, u32[]{:S(2)}) copy-start(s32[32]{0:T(128)S(1)} %get-tuple-element.5.depth_ref) | copy-start | bytes 388
  14.1 128.0 %all-gather.9.cloned.1.call-start = ((), (), s32[]{:S(2)}) async-start(), calls=%async_computation.2 | async-start | bytes 8912896 | tf_op jit(solution)/shard_map/all_gather | solution.py:151
  16.5 252.7 %all-gather.11.cloned.1.call-start = ((), (), s32[]{:S(2)}) async-start(), calls=%async_computation.3 | async-start | bytes 17825792 | tf_op jit(solution)/shard_map/all_gather | solution.py:152
Sparse Core Ops, SparseCore 0:
  8.9 22.3 all-gather.4
  32.8 33.0 all-gather.6
  68.1 73.9 all-gather.8
  144.1 125.0 all-gather.10

commit v2 on v1

--- a/solution.py
+++ b/solution.py
@@ -121,6 +121,150 @@
     return x.transpose(2, 1, 0).reshape(rows * channels, depth)
 
 
+MESH = pl.DeviceIdType.MESH
+Y_SIZE, CORES = 2, 2
+
+
+def gather_kernel(depth, width, pair_in, free_in, left_pair_in, left_free_in, pair_out, free_out, left_pair_out,
+                  left_free_out, send_sem, recv_sem, left_send, left_recv, local_sem):
+    row, col = lax.axis_index("row"), lax.axis_index("col")
+    core, y, z = row % CORES, (row // CORES) % Y_SIZE, row // (CORES * Y_SIZE)
+
+    def row_of(z_at, y_at, core_at):
+        return (z_at * Y_SIZE + y_at) * CORES + core_at
+
+    up, down = row_of(z + 1, y, core), row_of(z - 1, y, core)
+    across, sibling = row_of(z, 1 - y, core), row_of(z, y, 1 - core)
+    has_up, has_down = z < depth - 1, z > 0
+
+    barrier = pltpu.get_barrier_semaphore()
+
+    def greet(axis, at):
+        pl.semaphore_signal(barrier, inc=1, device_id={axis: at}, device_id_type=MESH)
+
+    pl.when(has_up)(lambda: greet("row", up))
+    pl.when(has_down)(lambda: greet("row", down))
+    greet("row", across)
+    greet("row", sibling)
+    for shift in range(1, width):
+        greet("col", lax.rem(col + shift, width))
+    pl.semaphore_wait(barrier, jnp.where(has_up, 1, 0) + jnp.where(has_down, 1, 0) + 2 + width - 1)
+
+    pieces = [(pair_in, pair_out, 0), (free_in, free_out, 0), (free_in, free_out, 1), (pair_in, pair_out, 1)]
+    early = {0}
+
+    def copy(piece, way, origin, target, own):
+        source, out, half = pieces[piece]
+        here = out.at[origin, half]
+        return pltpu.make_async_remote_copy(
+            src_ref=source.at[half] if own else here, dst_ref=here,
+            send_sem=send_sem.at[way, piece, origin // CORES], recv_sem=recv_sem.at[piece, origin],
+            device_id={"row": target}, device_id_type=MESH)
+
+    def forward(piece, z_at, y_at, started):
+        origin = row_of(z_at, y_at, core)
+        own_line = y_at is y
+        own = own_line and z_at is z
+        def go(way, target):
+            c = copy(piece, way, origin, target, own)
+            c.start() if started else c.wait_send()
+        if own_line or piece in early:
+            pl.when(has_up & (z_at <= z))(lambda: go(0, up))
+            pl.when(has_down & (z_at >= z))(lambda: go(1, down))
+        if own_line and (own or piece not in early):
+            go(2, across)
+        go(3, sibling)
+
+    def arrive(piece, z_at, y_at, core_at):
+        origin = row_of(z_at, y_at, core_at)
+        copy(piece, 3, origin, sibling, False).wait_recv()
+
+    for piece in range(len(pieces)):
+        forward(piece, z, y, True)
+
+    lefts = [(left_pair_in, left_pair_out), (left_free_in, left_free_out)]
+    left_copies = []
+    for n, (source, out) in enumerate(lefts):
+        for shift in range(1, width):
+            c = pltpu.make_async_remote_copy(
+                src_ref=source, dst_ref=out.at[col], send_sem=left_send.at[n, shift], recv_sem=left_recv.at[n, shift],
+                device_id={"col": lax.rem(col + shift, width)}, device_id_type=MESH)
+            c.start()
+            left_copies.append(c)
+    local = [
+        pltpu.make_async_copy(pair_in, pair_out.at[row], local_sem.at[0]),
+        pltpu.make_async_copy(free_in, free_out.at[row], local_sem.at[1]),
+        pltpu.make_async_copy(left_pair_in, left_pair_out.at[col], local_sem.at[2]),
+        pltpu.make_async_copy(left_free_in, left_free_out.at[col], local_sem.at[3]),
+    ]
+    for c in local:
+        c.start()
+
+    other = 1 - y
+
+    def hops(hop):
+        if hop == 0:
+            return ((z, None),)
+        return ((z - hop, z >= hop), (z + hop, z + hop < depth))
+
+    def sweep(hop, y_at):
+        for piece in range(len(pieces)):
+            for z_at, there in hops(hop):
+                def step(piece=piece, z_at=z_at):
+                    arrive(piece, z_at, y_at, core)
+                    forward(piece, z_at, y_at, True)
+                step() if there is None else pl.when(there)(step)
+
+    for hop in range(depth):
+        if hop > 0:
+            sweep(hop, y)
+        sweep(hop, other)
+
+    def every(do):
+        for piece in range(len(pieces)):
+            for hop in range(depth):
+                for z_at, there in hops(hop):
+                    for y_at in (y, other):
+                        step = functools.partial(do, piece, z_at, y_at)
+                        step() if there is None else pl.when(there)(step)
+
+    every(lambda piece, z_at, y_at: arrive(piece, z_at, y_at, 1 - core))
+    every(lambda piece, z_at, y_at: forward(piece, z_at, y_at, False))
+    for c in left_copies:
+        c.wait()
+    for c in local:
+        c.wait()
+
+
+def gather_all(right_pair, right_free, left_pair, left_free):
+    count, width = lax.axis_size("row"), lax.axis_size("col")
+    depth = count // (Y_SIZE * CORES)
+
+    def halved(x):
+        return x.reshape(2, x.shape[0] // 2, x.shape[1])
+
+    ins = (halved(right_pair), halved(right_free), left_pair, left_free)
+    counts = (count, count, width, width)
+    outs = pl.pallas_call(
+        functools.partial(gather_kernel, depth, width),
+        out_shape=[jax.ShapeDtypeStruct((n,) + x.shape, x.dtype) for n, x in zip(counts, ins)],
+        in_specs=[pl.BlockSpec(memory_space=pl.ANY)] * 4,
+        out_specs=[pl.BlockSpec(memory_space=pl.ANY)] * 4,
+        scratch_shapes=[
+            pltpu.SemaphoreType.DMA((4, 4, count // CORES)),
+            pltpu.SemaphoreType.DMA((4, count)),
+            pltpu.SemaphoreType.DMA((2, width)),
+            pltpu.SemaphoreType.DMA((2, width)),
+            pltpu.SemaphoreType.DMA((4,)),
+        ],
+        compiler_params=pltpu.CompilerParams(collective_id=0, has_side_effects=True),
+        name="gather_all",
+    )(*ins)
+    right = [x.reshape(-1, x.shape[-1]) for x in outs[:2]]
+    left = [x.transpose(1, 0, 2).reshape(x.shape[1], -1) for x in outs[2:]]
+    return (*right, *left)
+
+
 def body(
     paired_left, paired_right, unpaired_left, unpaired_right,
     out_weight, out_bias, chain_lengths, unpaired_depths,
@@ -148,10 +292,8 @@
     live = free_ids[:, None] < depth[None, :]
     masked = jnp.where(live[:, None, :], unpaired_left, jnp.zeros((), unpaired_left.dtype))
 
-    right_pair = lax.all_gather(flat_right(paired_right), "row", axis=0, tiled=True)
-    right_free = lax.all_gather(flat_right(unpaired_right), "row", axis=0, tiled=True)
-    left_pair = lax.all_gather(flat_left(paired_left), "col", axis=1, tiled=True)
-    left_free = lax.all_gather(flat_left(masked), "col", axis=1, tiled=True)
+    right_pair, right_free, left_pair, left_free = gather_all(
+        flat_right(paired_right), flat_right(unpaired_right), flat_left(paired_left), flat_left(masked))
 
     out_channels = out_weight.shape[1]
     weight = out_weight.reshape(channels, channels, out_channels).transpose(2, 1, 0).reshape(out_channels, -1)

time: 344 us -> 228 us (0.66); the launches traced: 339 us -> 228 us
  waiting for transfers between devices: 249 us -> 0 us
  Pallas kernels: 63.5 us -> 213 us
  between operations: 13.2 us -> 0.07 us
    all_gather x4 -> x0, waiting for transfers between devices: 249 us -> none  [the longest x1 127 us: body(): lax.all_gather(flat_right(unpaired_right), 'row', axis=0, tiled=True)]
    pallas_call x0 -> x1, Pallas kernels: none -> 144 us  [gather_all(): pl.pallas_call(functools.partial(gather_kernel, depth, width), out_shape=...]
    pallas_call x1, Pallas kernels: 63.5 us -> 68.5 us  [outer_product(): pl.pallas_call(functools.partial(outer_kernel, float(paired_total), group...]
  transfers between devices with their start and end apart: 4 -> 0, of which waited for: 4 -> 0; matrix products, arithmetic and copies ran while one was open for 3% -> 0% of each run, Pallas kernels for 0% -> 0%
where the time goes in v2:
time: 228 us
  Pallas kernels  213 us (93%)
  local copies, waits for them, and re-layouts  10.7 us (5%)
  other arithmetic  4.25 us (2%)
    pallas_call x1, Pallas kernels, gather_all(): pl.pallas_call(functools.partial(gather_kernel, depth, width), out_shape=...  144 us
    pallas_call x1, Pallas kernels, outer_product(): pl.pallas_call(functools.partial(outer_kernel, float(paired_total), group...  68.5 us

profile of v2, /device:TPU:5, one launch (start us, length us, event | category | flops | bytes accessed | tf_op | source)
XLA Modules:
  0.0 227.6 jit_solution(17633700917392522595)
XLA Ops:
  0.0 0.0 copy-start
  0.0 0.9 reduce-window.8
  0.9 0.7 bitcast_subtract_fusion
  1.6 0.7 select_reduce_fusion
  2.3 0.0 copy-start.5
  2.4 0.5 broadcast_subtract_fusion
  2.9 0.1 broadcast_compare_fusion
  3.0 1.3 select_bitcast_fusion
  4.3 1.6 copy.34
  5.9 0.0 copy-done.5
  5.9 0.0 copy-done
  5.9 0.2 bitcast_bitcast_fusion
  6.1 0.0 copy-start.3
  6.1 1.3 reshape_reshape.7.free_in
  7.4 0.0 copy-done.2
  7.4 0.1 bitcast_bitcast_fusion.1
  7.5 1.0 reshape_reshape.6.pair_in
  8.5 1.1 copy.33
  9.6 144.1 %gather_all.1 = (bf16[16,2,16,8192]{3,2,1,0:T(8,128)(2,1)}, bf16[16,2,32,8192]{3,2,1,0:T(8,128)(2,1)}, bf16[2,1024,256]{2,1,0:T(8,128)(2,1)}, bf16[2,1024,512]{2,1,0:T(8,128)(2,1)}) custom-call(bf16[2,16,8192]{2,1,0:T(8,128)(2,1)} %reshape_reshape.6.pair_in, bf16[2,32,8192]{2,1,0:T(8,128)(2,1)} %reshape_reshape.7.free_in, bf16[1024,256]{1,0:T(8,128)(2,1)} %bitcast.45, ...), custom_call_target="tpu_custom_call" | custom-call | tf_op jit(solution)/shard_map/gather_all/pallas_call | solution.py:248
  153.7 3.4 %copy.42 = bf16[2,128,8,512]{3,2,0,1:T(8,128)(2,1)} copy(bf16[2,128,8,512]{3,2,1,0:T(8,128)(2,1)} %bitcast.44) | data formatting | bytes 4194304 | tf_op jit(solution)/shard_map/reshape | solution.py:264
  157.1 1.1 copy.41
  158.2 0.1 copy.37
  158.3 0.8 copy.38.weight
  159.2 68.5 %outer_product.1 = bf16[32,256,128]{2,1,0:T(8,128)(2,1)} custom-call(s32[32]{0:T(128)} %get-tuple-element.17.start_ref, s32[32]{0:T(128)} %get-tuple-element.16.end_ref, s32[32]{0:T(128)} %copy-done.5, bf16[1024,512]{1,0:T(8,128)(2,1)} %bitcast.43, bf16[1024,1024]{1,0:T(8,128)(2,1)} %bitcast.41, bf16[512,8192]{1,0:T(8,128)(2,1)} %bitcast.40, ...), custom_call_target="tpu_custom_call" | custom-call | tf_op jit(solution)/shard_map/outer_product/pallas_call | solution.py:94
  (8 shorter events, 0.0 us)
Async XLA Ops:
  0.0 5.9 %copy-start = (bf16[64,32,256]{2,1,0:T(8,128)(2,1)S(1)}, bf16[64,32,256]{2,1,0:T(8,128)(2,1)}, u32[]{:S(2)}) copy-start(bf16[64,32,256]{2,1,0:T(8,128)(2,1)} %param.11) | copy-start | bytes 3145732
  2.3 3.6 %copy-start.5 = (s32[32]{0:T(128)}, s32[32]{0:T(128)S(1)}, u32[]{:S(2)}) copy-start(s32[32]{0:T(128)S(1)} %get-tuple-element.13.depth_ref) | copy-start | bytes 388
  5.9 1.5 copy-start.2
  6.1 2.4 %copy-start.3 = (bf16[256,32,32]{0,2,1:T(8,128)(2,1)S(1)}, bf16[256,32,32]{0,2,1:T(8,128)(2,1)}, u32[]{:S(2)}) copy-start(bf16[256,32,32]{0,2,1:T(8,128)(2,1)} %param.8) | copy-start | bytes 1572868
  153.7 3.4 %copy-start.1 = (bf16[2,1024,256]{2,1,0:T(8,128)(2,1)S(1)}, bf16[2,1024,256]{2,1,0:T(8,128)(2,1)}, u32[]{:S(2)}) copy-start(bf16[2,1024,256]{2,1,0:T(8,128)(2,1)} %get-tuple-element.9) | copy-start | bytes 3145732
  157.1 1.1 copy-start.4

commit v3 on v2

--- a/solution.py
+++ b/solution.py
@@ -8,7 +8,7 @@
 from jax.sharding import PartitionSpec as P
 
 LANES = 128
-D_STEP = 8
+D_STEP = 16
 
 
 def outer_kernel(
@@ -19,22 +19,29 @@
 ):
     tile, step = pl.program_id(0), pl.program_id(1)
     rows = start_ref.shape[0]
-    channels = left_pair.shape[0] // rows
+    channels = left_pair.shape[1] // rows
     width = right_pair.shape[1]
     d_step = width // LANES
     lanes = lax.broadcasted_iota(jnp.int32, (1, LANES), 1) + tile * LANES
     span = group * channels
 
+    @pl.when(step == 0)
+    def _():
+        acc[...] = jnp.zeros_like(acc)
+
+    def left(ref, at):
+        return jnp.concatenate([ref[n, at, :] for n in range(ref.shape[0])], axis=1)
+
     @pl.loop(0, rows // group)
     def _(g):
         base = g * group
         at = pl.ds(pl.multiple_of(base * channels, span), span)
-        outer_scr[...] = jnp.dot(left_pair[at, :], right_pair[...], preferred_element_type=jnp.float32)
+        outer_scr[...] = jnp.dot(left(left_pair, at), right_pair[...], preferred_element_type=jnp.float32)
         first, last = start_ref[base], end_ref[base + group - 1]
 
         @pl.when((first < (tile + 1) * LANES) & (last > tile * LANES))
         def _():
-            free_scr[...] = jnp.dot(left_free[at, :], right_free[...], preferred_element_type=jnp.float32)
+            free_scr[...] = jnp.dot(left(left_free, at), right_free[...], preferred_element_type=jnp.float32)
             for i in range(group):
                 same = (lanes >= start_ref[base + i]) & (lanes < end_ref[base + i])
                 part = pl.ds(i * channels, channels)
@@ -51,16 +58,7 @@
             projected = jnp.dot(
                 weight[...], jnp.concatenate(halves, axis=1), preferred_element_type=jnp.float32)
             for k in range(2):
-                row = base + 2 * pair + k
-                value = projected[:, k * LANES:(k + 1) * LANES]
-
-                @pl.when(step == 0)
-                def _():
-                    acc[row] = value
-
-                @pl.when(step > 0)
-                def _():
-                    acc[row] += value
+                acc[base + 2 * pair + k] += projected[:, k * LANES:(k + 1) * LANES]
 
     @pl.when(step == pl.num_programs(1) - 1)
     def _():
@@ -69,7 +67,7 @@
             same = (lanes >= start_ref[i]) & (lanes < end_ref[i])
             depth = depth_ref[i].astype(jnp.float32)
             count = paired_total + jnp.where(same, depth, 0.0)
-            value = (acc[i] / count).T
+            value = (acc[i] * (1.0 / count)).T
             if final:
                 value = value + bias[...]
             out_ref[i] = value.astype(out_ref.dtype)
@@ -77,7 +75,7 @@
 
 def outer_product(left_pair, left_free, right_pair, right_free, weight, bias, start, end, depth, paired_total, final):
     rows = start.shape[0]
-    channels = left_pair.shape[0] // rows
+    channels = left_pair.shape[1] // rows
     out_channels = weight.shape[0]
     cols = right_pair.shape[1] // channels
     group = min(16, rows)
@@ -86,7 +84,7 @@
     smem = pl.BlockSpec(memory_space=pltpu.SMEM)
 
     def whole(x):
-        return pl.BlockSpec(x.shape, lambda t, s: (0, 0))
+        return pl.BlockSpec(x.shape, lambda t, s: (0,) * x.ndim)
 
     def streamed(x):
         return pl.BlockSpec((x.shape[0], width), lambda t, s: (0, t * steps + s))
@@ -261,8 +259,7 @@
         name="gather_all",
     )(*ins)
     right = [x.reshape(-1, x.shape[-1]) for x in outs[:2]]
-    left = [x.transpose(1, 0, 2).reshape(x.shape[1], -1) for x in outs[2:]]
-    return (*right, *left)
+    return (*right, *outs[2:])
 
 
 def body(
@@ -274,7 +271,9 @@
     first_row = lax.axis_index("row") * rows
     first_col = lax.axis_index("col") * cols
     positions = first_row + jnp.arange(rows, dtype=jnp.int32)
-    chain_ends = jnp.cumsum(chain_lengths)
+    chains = jnp.arange(chain_lengths.shape[0])
+    chain_ends = jnp.sum(
+        jnp.where(chains[None, :] <= chains[:, None], chain_lengths[None, :], 0), axis=1, dtype=jnp.int32)
     chain_starts = chain_ends - chain_lengths
     inside = (positions[:, None] >= chain_starts[None, :]) & (positions[:, None] < chain_ends[None, :])
 

time: 228 us -> 201 us (0.88)
  Pallas kernels: 213 us -> 190 us
  local copies, waits for them, and re-layouts: 10.7 us -> 6.26 us
    pallas_call x1, Pallas kernels: 68.5 us -> 46.1 us  [outer_product(): pl.pallas_call(functools.partial(outer_kernel, float(paired_total), group...]
    reshape x2 -> x0, local copies, waits for them, and re-layouts: 4.45 us -> none  [gather_all(): left = [x.transpose(1, 0, 2).reshape(x.shape[1], -1) for x in outs[2:]]]
where the time goes in v3:
time: 201 us
  Pallas kernels  190 us (95%)
  local copies, waits for them, and re-layouts  6.26 us (3%)
  other arithmetic  4.25 us (2%)
    pallas_call x1, Pallas kernels, gather_all(): pl.pallas_call(functools.partial(gather_kernel, depth, width), out_shape=...  144 us
    pallas_call x1, Pallas kernels, outer_product(): pl.pallas_call(functools.partial(outer_kernel, float(paired_total), group...  46.1 us

profile of v3, /device:TPU:5, one launch (start us, length us, event | category | flops | bytes accessed | tf_op | source)
XLA Modules:
  0.0 200.8 jit_solution(8282586771837641847)
XLA Ops:
  0.0 0.0 copy-start
  0.0 0.0 copy-start.3
  0.0 0.9 select_reduce_fusion.3
  1.0 0.7 sub.13
  1.6 0.7 select_reduce_fusion
  2.4 0.0 copy-start.4
  2.4 0.5 broadcast_subtract_fusion
  2.9 0.1 broadcast_compare_fusion
  3.0 1.3 select_bitcast_fusion
  4.3 1.5 copy.28
  5.9 0.0 copy-done
  5.9 0.2 bitcast_bitcast_fusion
  6.1 1.3 reshape_reshape.7.free_in
  7.3 0.0 copy-done.1
  7.3 0.1 bitcast_bitcast_fusion.1
  7.4 1.0 reshape_reshape.6.pair_in
  8.5 0.0 copy-done.2
  8.5 1.1 copy.27
  9.6 144.1 %gather_all.1 = (bf16[16,2,16,8192]{3,2,1,0:T(8,128)(2,1)}, bf16[16,2,32,8192]{3,2,1,0:T(8,128)(2,1)}, bf16[2,1024,256]{2,1,0:T(8,128)(2,1)}, bf16[2,1024,512]{2,1,0:T(8,128)(2,1)}) custom-call(bf16[2,16,8192]{2,1,0:T(8,128)(2,1)} %reshape_reshape.6.pair_in, bf16[2,32,8192]{2,1,0:T(8,128)(2,1)} %reshape_reshape.7.free_in, bf16[1024,256]{1,0:T(8,128)(2,1)} %bitcast.33, ...), custom_call_target="tpu_custom_call" | custom-call | tf_op jit(solution)/shard_map/gather_all/pallas_call | solution.py:246
  153.7 0.0 copy-done.3
  153.8 0.1 copy.29
  153.9 0.8 copy.30.weight
  154.7 0.0 copy-done.4
  154.7 46.1 %outer_product.1 = bf16[32,256,128]{2,1,0:T(8,128)(2,1)} custom-call(s32[32]{0:T(128)} %get-tuple-element.17.start_ref, s32[32]{0:T(128)} %get-tuple-element.16.end_ref, s32[32]{0:T(128)} %copy-done.4, bf16[2,1024,256]{2,1,0:T(8,128)(2,1)} %get-tuple-element.9.left_pair, bf16[2,1024,512]{2,1,0:T(8,128)(2,1)} %get-tuple-element.10.left_free, ...), custom_call_target="tpu_custom_call" | custom-call | tf_op jit(solution)/shard_map/outer_product/pallas_call | solution.py:92
  (4 shorter events, 0.0 us)
Async XLA Ops:
  0.0 5.9 %copy-start = (bf16[64,32,256]{2,1,0:T(8,128)(2,1)S(1)}, bf16[64,32,256]{2,1,0:T(8,128)(2,1)}, u32[]{:S(2)}) copy-start(bf16[64,32,256]{2,1,0:T(8,128)(2,1)} %param.11) | copy-start | bytes 3145732
  0.0 7.3 %copy-start.1 = (bf16[32,32,256]{2,1,0:T(8,128)(2,1)S(1)}, bf16[32,32,256]{2,1,0:T(8,128)(2,1)}, u32[]{:S(2)}) copy-start(bf16[32,32,256]{2,1,0:T(8,128)(2,1)} %param.9) | copy-start | bytes 1572868
  0.0 8.5 %copy-start.2 = (bf16[256,32,32]{0,2,1:T(8,128)(2,1)S(1)}, bf16[256,32,32]{0,2,1:T(8,128)(2,1)}, u32[]{:S(2)}) copy-start(bf16[256,32,32]{0,2,1:T(8,128)(2,1)} %param.8) | copy-start | bytes 1572868
  0.0 153.7 %copy-start.3 = (bf16[1024,128]{1,0:T(8,128)(2,1)S(1)}, bf16[1024,128]{1,0:T(8,128)(2,1)}, u32[]{:S(2)}) copy-start(bf16[1024,128]{1,0:T(8,128)(2,1)} %param.12) | copy-start | bytes 786436
  2.4 152.3 %copy-start.4 = (s32[32]{0:T(128)}, s32[32]{0:T(128)S(1)}, u32[]{:S(2)}) copy-start(s32[32]{0:T(128)S(1)} %get-tuple-element.13.depth_ref) | copy-start | bytes 388
